TPU v7x, 32 devices: a whole 2x2x4 slice. The times are simulated.
32 devices in a mesh: dp: 4 (over x, core), tensor: 8 (over z, y).
Axes of the slice: x: 2, y: 2, z: 4, core: 2. Of those that a mesh axis runs over, the one named last changes fastest.
Arguments:
- grad_out: bfloat16 [256, 4096], P(('dp', 'tensor')), may hold values from -6 to 6
- gate_pre: bfloat16 [256, 14848], P('dp', 'tensor'), may hold values from -8 to 8
- up_pre: bfloat16 [256, 14848], P('dp', 'tensor'), may hold values from -6 to 6
- down_weight: bfloat16 [4096, 14848], P(None, 'tensor'), may hold values from -1.5 to 1.5
Outputs:
- grad_weight: float32 [4096, 14848], P('dp', 'tensor')
- grad_gate: bfloat16 [256, 14848], P('dp', 'tensor')
- grad_up: bfloat16 [256, 14848], P('dp', 'tensor')
All inputs are finite; a program needn't handle non-finite values.
Results may differ from a plain program's by a relative error of at most 0.015.
Values may be sent and summed in bfloat16 or wider, within the bound.
A program may use at most 128 MiB of HBM per device.

v0:
```python
import functools

import jax
import jax.numpy as jnp
from jax import lax
from jax.experimental import pallas as pl
from jax.experimental.pallas import tpu as pltpu
from jax.sharding import PartitionSpec as P

MESH = pl.DeviceIdType.MESH
CORES = 2
PARTS = 2
VMEM = 67043328


def gather_kernel(
    n_dp, n_t, outer, widths,
    go_hbm, gate_hbm, up_hbm, weight_hbm,
    cols_ref, hidden_ref, grad_ref,
    rows, gate, upper, weight, left,
    load_sem, weight_sem, send_sem,
    rows_sem, cross_sem, line_sem, hidden_sem, pair_sem,
):
    inner = n_t // outer
    n_chip = n_dp // CORES
    depth = go_hbm.shape[0]
    feats = cols_ref.shape[-1]
    share = go_hbm.shape[1] // PARTS
    parts = [pl.ds(h * share, share) for h in range(PARTS)]
    dp, t = lax.axis_index("dp"), lax.axis_index("tensor")
    chip, core = dp // CORES, dp % CORES
    mate = chip * CORES + (1 - core)
    a, b = t // inner, t % inner
    chips = [lax.rem(chip + d, n_chip) for d in range(1, n_chip)]
    lines = [lax.rem(a + d, outer) * inner + b for d in range(1, outer)]
    sides = [a * inner + lax.rem(b + d, inner) for d in range(1, inner)]

    loads = [
        pltpu.make_async_copy(go_hbm, rows.at[t], load_sem.at[0]),
        pltpu.make_async_copy(gate_hbm, gate, load_sem.at[1]),
        pltpu.make_async_copy(up_hbm, upper, load_sem.at[2]),
    ]
    for load in loads:
        load.start()
    weight_loads = []
    start = 0
    for k, width in enumerate(widths):
        span = pl.ds(start, width)
        weight_loads.append(pltpu.make_async_copy(weight_hbm.at[span], weight.at[span], weight_sem.at[k]))
        weight_loads[-1].start()
        start += width

    barrier = pltpu.get_barrier_semaphore()
    peers = [(lax.rem(dp + d, n_dp), t) for d in range(1, n_dp)]
    peers += [(dp, other) for other in lines + sides]
    for peer in peers:
        pl.semaphore_signal(barrier, inc=1, device_id=peer, device_id_type=MESH)
    loads[0].wait()
    pl.semaphore_wait(barrier, len(peers))

    sent = []

    def send(src, dst, sem, peer):
        copy = pltpu.make_async_remote_copy(
            src_ref=src, dst_ref=dst, send_sem=send_sem.at[len(sent)], recv_sem=sem,
            device_id=peer, device_id_type=MESH,
        )
        copy.start()
        sent.append(copy)

    def arrived(dst, sem):
        pltpu.make_async_remote_copy(
            src_ref=dst, dst_ref=dst, send_sem=send_sem.at[0], recv_sem=sem,
            device_id=(mate, t), device_id_type=MESH,
        ).wait_recv()

    def block_of(group):
        return pl.ds(pl.multiple_of(group * feats, feats), feats)

    for other in chips:
        for c in range(CORES):
            group = other * CORES + c
            send(rows.at[t, :, block_of(group)], cols_ref.at[chip, core, t], cross_sem.at[chip, core], (group, t))
    for h, part in enumerate(parts):
        mine = rows.at[t, :, part]
        for peer in lines + sides:
            send(mine, mine, rows_sem.at[h, t], (dp, peer))

    loads[1].wait()
    loads[2].wait()
    g = gate[...].astype(jnp.float32)
    u = upper[...].astype(jnp.float32)
    hidden_ref[chip, core] = (g * jax.nn.sigmoid(g) * u).astype(jnp.bfloat16)
    mine = hidden_ref.at[chip, core]
    for other in chips:
        send(mine, mine, hidden_sem.at[chip, core], (other * CORES + core, t))
    send(mine, mine, hidden_sem.at[chip, core], (mate, t))

    for other in chips:
        for c in range(CORES):
            arrived(cols_ref.at[other, c, t], cross_sem.at[other, c])
        block = cols_ref.at[other, :, t]
        for peer in lines + sides:
            send(block, block, line_sem.at[other, t], (dp, peer))

    for h, part in enumerate(parts):
        for source in lines:
            block = rows.at[source, :, part]
            arrived(block, rows_sem.at[h, source])
            for side in sides:
                send(block, block, rows_sem.at[h, source], (dp, side))

    for other in chips:
        block = hidden_ref.at[other, core]
        arrived(block, hidden_sem.at[other, core])
        send(block, block, hidden_sem.at[other, core], (mate, t))

    def pass_on(source):
        for other in chips:
            block = cols_ref.at[other, :, source]
            arrived(block, line_sem.at[other, source])
            for side in sides:
                send(block, block, line_sem.at[other, source], (dp, side))

    from_sides = [
        step * inner + lax.rem(b + d, inner)
        for step in range(outer) for d in range(1, inner)
    ]
    waiting = list(lines)
    for h, part in enumerate(parts):
        for source in from_sides:
            arrived(rows.at[source, :, part], rows_sem.at[h, source])
        if h == PARTS - 1:
            send(rows.at[:, :, block_of(mate)], cols_ref.at[chip, core], pair_sem.at[0], (mate, t))
            keep = pltpu.make_async_copy(rows.at[:, :, block_of(dp)], cols_ref.at[chip, core], load_sem.at[3])
            keep.start()
        left[:, part] = rows[:, :, part].astype(jnp.float32).reshape(n_t * depth, share).astype(jnp.bfloat16)
        start = 0
        for k, width in enumerate(widths):
            if h == 0:
                weight_loads[k].wait()
            span = pl.ds(start, width)
            term = lax.dot_general(
                left[:, part], weight[span, part], (((1,), (1,)), ((), ())), preferred_element_type=jnp.float32
            )
            grad_ref[:, span] = term if h == 0 else grad_ref[:, span] + term
            start += width
            if waiting:
                pass_on(waiting.pop(0))
    while waiting:
        pass_on(waiting.pop(0))

    for source in from_sides:
        for other in chips:
            arrived(cols_ref.at[other, :, source], line_sem.at[other, source])
    for other in chips + [chip]:
        arrived(hidden_ref.at[other, 1 - core], hidden_sem.at[other, 1 - core])
    arrived(cols_ref.at[chip, 1 - core], pair_sem.at[0])
    keep.wait()
    for copy in sent:
        copy.wait_send()


def finish_kernel(cols_ref, hidden_ref, grad_ref, gate_ref, up_ref, weight_out, gate_out, up_out):
    weight_out[...] = lax.dot_general(
        hidden_ref[...], cols_ref[...], (((0,), (0,)), ((), ())), preferred_element_type=jnp.float32
    )
    grad = grad_ref[...]
    gate = gate_ref[...].astype(jnp.float32)
    upper = up_ref[...].astype(jnp.float32)
    sig = jax.nn.sigmoid(gate)
    up_out[...] = (grad * (gate * sig)).astype(jnp.bfloat16)
    gate_out[...] = (grad * upper * sig * (1.0 + gate * (1.0 - sig))).astype(jnp.bfloat16)


def body(n_dp, n_t, grad_out, gate_pre, up_pre, down_weight):
    depth, model = grad_out.shape
    group, wide = gate_pre.shape
    feats = model // n_dp
    n_chip = n_dp // CORES
    outer = 4 if n_t % 4 == 0 else 1
    inner = n_t // outer
    step = 512
    widths = [min(step, wide - start) for start in range(0, wide, step)]
    n_send = (
        (n_chip - 1) * CORES + (outer * inner - 1) * (n_chip - 1 + PARTS) + 2 * n_chip
    )
    lanes = pl.cdiv(wide, 128) * 128
    results = 2 * n_dp * group * (feats + lanes) + 4 * group * lanes
    anywhere = pl.BlockSpec(memory_space=pltpu.HBM)
    vmem = pl.BlockSpec(memory_space=pltpu.VMEM)
    dma = pltpu.SemaphoreType.DMA
    cols, hidden, grad = pl.pallas_call(
        functools.partial(gather_kernel, n_dp, n_t, outer, widths),
        out_shape=[
            jax.ShapeDtypeStruct((n_chip, CORES, n_t, depth, feats), jnp.bfloat16),
            jax.ShapeDtypeStruct((n_chip, CORES, group, wide), jnp.bfloat16),
            jax.ShapeDtypeStruct((group, wide), jnp.float32),
        ],
        in_specs=[anywhere] * 4,
        out_specs=[vmem] * 3,
        scratch_shapes=[
            pltpu.VMEM((n_t, depth, model), jnp.bfloat16),
            pltpu.VMEM((group, wide), jnp.bfloat16),
            pltpu.VMEM((group, wide), jnp.bfloat16),
            pltpu.VMEM((wide, model), jnp.bfloat16),
            pltpu.VMEM((group, model), jnp.bfloat16),
            dma((4,)),
            dma((len(widths),)),
            dma((n_send,)),
            dma((PARTS, n_t)),
            dma((n_chip, CORES)),
            dma((n_chip, n_t)),
            dma((n_chip, CORES)),
            dma((1,)),
        ],
        compiler_params=pltpu.CompilerParams(
            collective_id=0, has_side_effects=True, vmem_limit_bytes=VMEM - results - 16 * 1024
        ),
    )(grad_out, gate_pre, up_pre, down_weight.T)
    cols = cols.reshape(n_dp * group, feats)
    hidden = hidden.reshape(n_dp * group, wide)

    tile = 512
    tiles = pl.BlockSpec((group, tile), lambda i: (0, i))
    turned, grad_gate, grad_up = pl.pallas_call(
        finish_kernel,
        grid=(pl.cdiv(wide, tile),),
        out_shape=[
            jax.ShapeDtypeStruct((wide, feats), jnp.float32),
            jax.ShapeDtypeStruct((group, wide), jnp.bfloat16),
            jax.ShapeDtypeStruct((group, wide), jnp.bfloat16),
        ],
        in_specs=[
            pl.BlockSpec((n_dp * group, feats), lambda i: (0, 0)),
            pl.BlockSpec((n_dp * group, tile), lambda i: (0, i)),
            tiles, tiles, tiles,
        ],
        out_specs=[pl.BlockSpec((tile, feats), lambda i: (i, 0)), tiles, tiles],
        compiler_params=pltpu.CompilerParams(vmem_limit_bytes=VMEM - results - 16 * 1024),
    )(cols, hidden, grad, gate_pre, up_pre)
    return turned.T, grad_gate, grad_up


def solution(mesh):
    in_specs = (P(("dp", "tensor"), None), P("dp", "tensor"), P("dp", "tensor"), P(None, "tensor"))
    out_specs = (P("dp", "tensor"), P("dp", "tensor"), P("dp", "tensor"))
    fn = functools.partial(body, mesh.shape["dp"], mesh.shape["tensor"])
    return jax.shard_map(fn, mesh=mesh, in_specs=in_specs, out_specs=out_specs, check_vma=False)
```

profile of v0, /device:TPU:0, one launch (start us, length us, event | category | flops | bytes accessed | tf_op | source)
XLA Modules:
  0.0 29.8 jit_solution(10601026288652876305)
XLA Ops:
  0.6 23.1 %shard_map.67 = (bf16[2,2,8,8,1024]{4,3,2,1,0:T(8,128)(2,1)}, bf16[2,2,64,1856]{3,2,1,0:T(8,128)(2,1)}, f32[64,1856]{1,0:T(8,128)}) custom-call(bf16[8,4096]{1,0:T(8,128)(2,1)} %go_hbm.1, bf16[64,1856]{1,0:T(8,128)(2,1)} %gate_ref.1, bf16[64,1856]{1,0:T(8,128)(2,1)} %up_ref.1, bf16[1856,4096]{1,0:T(8,128)(2,1)} %bitcast.4), custom_call_target="tpu_custom_call" | custom-call | tf_op jit(solution)/shard_map/pallas_call | solution.py:193
  23.7 6.1 %shard_map.68 = (f32[1856,1024]{1,0:T(8,128)}, bf16[64,1856]{1,0:T(8,128)(2,1)}, bf16[64,1856]{1,0:T(8,128)(2,1)}) custom-call(bf16[256,1024]{1,0:T(8,128)(2,1)} %bitcast.6, bf16[256,1856]{1,0:T(8,128)(2,1)} %bitcast.5, f32[64,1856]{1,0:T(8,128)} %get-tuple-element.11.grad_ref, bf16[64,1856]{1,0:T(8,128)(2,1)} %gate_ref.1, bf16[64,1856]{1,0:T(8,128)(2,1)} %up_ref.1), custom_call_target="tpu_custom_call" | custom-call | tf_op jit(solution)/shard_map/pallas_call | solution.py:226
where the time goes:
time: 30 us; the launch traced here: 29.8 us
  Pallas kernels  29.2 us (97%)
  between operations  0.64 us (2%)
    pallas_call x1, Pallas kernels, body(): pl.pallas_call(functools.partial(gather_kernel, n_dp, n_t, outer, widths)...  23.1 us
    pallas_call x1, Pallas kernels, body(): pl.pallas_call(finish_kernel, grid=(pl.cdiv(wide, tile),), out_shape=[jax...  6.14 us

commit v1 on v0

v1 whole, which is shorter than its diff:
```python
import functools

import jax
import jax.numpy as jnp
from jax import lax
from jax.experimental import pallas as pl
from jax.experimental.pallas import tpu as pltpu
from jax.sharding import PartitionSpec as P

MESH = pl.DeviceIdType.MESH
CORES = 2
VMEM = 67043328


def cut(wide, step):
    return [(start, min(step, wide - start)) for start in range(0, wide, step)]


def gather_kernel(
    n_dp, n_t, outer, spans, pieces,
    go_hbm, gate_hbm, up_hbm, weight_hbm,
    cols_ref, hidden_ref, grad_ref, other_ref, act_ref, slope_ref,
    mine, extra, gate, upper, weight, left, acc, leave,
    load_sem, weight_sem, send_sem,
    own_sem, extra_sem, cross_sem, cols_sem, far_sem, hidden_sem, pair_sem, grad_sem,
):
    inner = n_t // outer
    n_chip = n_dp // CORES
    depth, feats = mine.shape[0], cols_ref.shape[-1]
    dp, t = lax.axis_index("dp"), lax.axis_index("tensor")
    chip, core = dp // CORES, dp % CORES
    mate = chip * CORES + (1 - core)
    a, b = t // inner, t % inner
    chips = [lax.rem(chip + d, n_chip) for d in range(1, n_chip)]
    sides = [lax.rem(b + d, inner) for d in range(1, inner)]

    has_line = outer == 4
    between = (a * (3 - a)) // 2
    twin, mirror, across = a + 1 - 2 * (a % 2), 3 - a, (a + 2) % 4
    first = between * mirror + (1 - between) * twin
    second = between * twin + (1 - between) * mirror
    line = [first, second, across] if has_line else []

    def at(step, side):
        return step * inner + side

    loads = [
        pltpu.make_async_copy(go_hbm, mine, load_sem.at[0]),
        pltpu.make_async_copy(gate_hbm, gate, load_sem.at[1]),
        pltpu.make_async_copy(up_hbm, upper, load_sem.at[2]),
    ]
    for load in loads:
        load.start()

    barrier = pltpu.get_barrier_semaphore()
    peers = [(lax.rem(dp + d, n_dp), t) for d in range(1, n_dp)]
    for c in range(CORES):
        peers += [(chip * CORES + c, at(step, b)) for step in line]
        peers += [(chip * CORES + c, at(a, side)) for side in sides]
    for peer in peers:
        pl.semaphore_signal(barrier, inc=1, device_id=peer, device_id_type=MESH)
    with jax.named_scope("go"):
        loads[0].wait()
    with jax.named_scope("barrier"):
        pl.semaphore_wait(barrier, len(peers))

    sent = []

    def copy_to(block, sem, peer, dst=None, slot=None):
        copy = pltpu.make_async_remote_copy(
            src_ref=block, dst_ref=block if dst is None else dst,
            send_sem=send_sem.at[len(sent) if slot is None else slot], recv_sem=sem,
            device_id=peer, device_id_type=MESH,
        )
        if slot is None:
            sent.append(copy)
        return copy

    def send(block, sem, peer, dst=None):
        copy_to(block, sem, peer, dst).start()

    def send_two(block, sem, peers, dst=None):
        slot = len(sent)
        for peer in peers:
            copy_to(block, sem, peer, dst, slot).start()
        sent.append(copy_to(cols_ref.at[chip, :, t], sem, peers[0], None, slot))

    def arrived(block, sem):
        pltpu.make_async_remote_copy(
            src_ref=block, dst_ref=block, send_sem=send_sem.at[0], recv_sem=sem,
            device_id=(mate, t), device_id_type=MESH,
        ).wait_recv()

    def block_of(group):
        return pl.ds(pl.multiple_of(group * feats, feats), feats)

    def spread(block, sem, group, dst=None):
        slot = None
        if has_line:
            send_two(block, sem, [(group, at(twin, b)), (group, at(mirror, b))], dst)
            slot = len(sent)
            last = copy_to(block, sem, (group, at(across, b)), dst)

            @pl.when(between == 0)
            def _():
                last.start()
        return slot

    def relay(block, sem, slot):
        @pl.when(between == 1)
        def _():
            copy_to(block, sem, (dp, at(twin, b)), slot=slot).start()

    for other in chips:
        for c in range(CORES):
            group = other * CORES + c
            send(mine.at[:, block_of(group)], cross_sem.at[chip, core], (group, t), cols_ref.at[chip, core, t])

    def own_block(source, dst, sem):
        slots = []
        for c in range(CORES):
            group = chip * CORES + c
            block = mine.at[:, block_of(source * CORES + c)]
            for side in sides:
                send(block, sem, (group, at(a, side)), dst)
            slots.append(spread(block, sem, group, dst))
        send(mine.at[:, block_of(source * CORES + 1 - core)], sem, (mate, t), dst)
        return slots

    own_slots = own_block(chip, cols_ref.at[chip, core, t], own_sem.at[t])
    extra_slots = [own_block(other, extra.at[other, core, t], extra_sem.at[other, core, t]) for other in chips]

    with jax.named_scope("hid_load"):
        loads[1].wait()
        loads[2].wait()
    kinds = [chip] + chips
    weight_loads = [
        [
            pltpu.make_async_copy(
                weight_hbm.at[pl.ds(start, width), block_of(kind * CORES + core)],
                weight.at[n, pl.ds(start, width)], weight_sem.at[n, k],
            )
            for k, (start, width) in enumerate(spans)
        ]
        for n, kind in enumerate(kinds)
    ]
    with jax.named_scope("hid"):
        g = gate[...].astype(jnp.float32)
        u = upper[...].astype(jnp.float32)
        sig = jax.nn.sigmoid(g)
        hidden_ref[chip, core] = (g * sig * u).astype(jnp.bfloat16)
        act_ref[...] = g * sig
        slope_ref[...] = u * sig * (1.0 + g * (1.0 - sig))
    for k, (start, width) in enumerate(pieces):
        piece = hidden_ref.at[chip, core, :, pl.ds(start, width)]
        for other in chips:
            send(piece, hidden_sem.at[k, chip, core], (other * CORES + core, t))
    send(hidden_ref.at[chip, core], pair_sem.at[0], (mate, t))
    for loads_of in weight_loads:
        for load in loads_of:
            load.start()
    cols_ref[chip, core, t] = mine[:, block_of(dp)]
    for other in chips:
        extra[other, core, t] = mine[:, block_of(other * CORES + core)]

    def own_line(i):
        source = at(line[i], b)
        block = cols_ref.at[chip, :, source]
        arrived(block, own_sem.at[source])
        if i == 0:
            for c in range(CORES):
                relay(cols_ref.at[chip, c, source], own_sem.at[source], own_slots[c])
        for side in sides:
            send(block, own_sem.at[source], (dp, at(a, side)))

    def extra_line(i):
        source = at(line[i], b)
        for n, other in enumerate(chips):
            for c in range(CORES):
                block = extra.at[other, c, source]
                arrived(block, extra_sem.at[other, c, source])
                if i == 0:
                    relay(block, extra_sem.at[other, c, source], extra_slots[n][c])
                if c == 0:
                    for side in sides:
                        send(block, extra_sem.at[other, c, source], (dp, at(a, side)))
            if i == 2:
                block = extra.at[other, :, source]
                send(block, far_sem.at[chip, b], (other * CORES + core, t), cols_ref.at[chip, :, source])

    def extra_side():
        slots = []
        for side in sides:
            for other in chips:
                source = at(a, side)
                block = extra.at[other, 1, source]
                arrived(block, extra_sem.at[other, 1, source])
                slots.append(spread(block, extra_sem.at[other, 1, source], dp))
        return slots

    def extra_relay():
        n = 0
        for side in sides:
            for other in chips:
                source = at(mirror, side)
                block, sem = extra.at[other, 1, source], extra_sem.at[other, 1, source]

                @pl.when(between == 1)
                def _():
                    arrived(block, sem)

                relay(block, sem, side_slots[n])
                n += 1

    def own_last():
        for side in sides:
            for step in [a] + line:
                source = at(step, side)
                arrived(cols_ref.at[chip, :, source], own_sem.at[source])
        arrived(cols_ref.at[chip, 1 - core, t], own_sem.at[t])

    def extra_last():
        for side in sides:
            for other in chips:
                arrived(extra.at[other, 0, at(a, side)], extra_sem.at[other, 0, at(a, side)])
                for i, step in enumerate(line):
                    source = at(step, side)
                    arrived(extra.at[other, 0, source], extra_sem.at[other, 0, source])
                    block, sem = extra.at[other, 1, source], extra_sem.at[other, 1, source]
                    if i == 0:

                        @pl.when(between == 0)
                        def _():
                            arrived(block, sem)
                    else:
                        arrived(block, sem)
                    if i == 2:
                        block = extra.at[other, :, source]
                        send(block, far_sem.at[chip, side], (other * CORES + core, t), cols_ref.at[chip, :, source])
        for other in chips:
            arrived(extra.at[other, 1 - core, t], extra_sem.at[other, 1 - core, t])

    def cols_own():
        for other in chips:
            for c in range(CORES):
                arrived(cols_ref.at[other, c, t], cross_sem.at[other, c])
            block = cols_ref.at[other, :, t]
            for side in sides:
                send(block, cols_sem.at[0, other, t], (dp, at(a, side)))
            if has_line:
                for step in (twin, mirror):
                    send(block, cols_sem.at[0, other, t], (dp, at(step, b)))

    def cols_line(i):
        source = at(line[i], b)
        for other in chips:
            sem = cols_sem.at[0, other, source]
            arrived(cols_ref.at[other, :, source], sem)
            for side in sides:
                send(cols_ref.at[other, 0, source], sem, (dp, at(a, side)))

    def cols_side():
        for side in sides:
            for other in chips:
                source = at(a, side)
                arrived(cols_ref.at[other, :, source], cols_sem.at[0, other, source])
                if has_line:
                    send_two(
                        cols_ref.at[other, 1, source], cols_sem.at[1, other, source], [(dp, at(twin, b)), (dp, at(mirror, b))]
                    )

    def cols_last():
        for other in chips:
            for side in sides:
                for step in line[:2]:
                    source = at(step, side)
                    arrived(cols_ref.at[other, 0, source], cols_sem.at[0, other, source])
                    arrived(cols_ref.at[other, 1, source], cols_sem.at[1, other, source])
            if has_line:
                for side in [b] + sides:
                    source = at(across, side)
                    arrived(cols_ref.at[other, :, source], far_sem.at[other, side])

    def hidden_piece(k):
        start, width = pieces[k]
        for other in chips:
            piece = hidden_ref.at[other, core, :, pl.ds(start, width)]
            arrived(piece, hidden_sem.at[k, other, core])
            send(piece, hidden_sem.at[k, other, core], (mate, t))

    def scoped(name, job, *args):
        with jax.named_scope(name):
            return job(*args)

    if has_line:
        scoped("own_line0", own_line, 0)
        scoped("own_line1", own_line, 1)
    side_slots = scoped("extra_side", extra_side)
    if has_line:
        scoped("own_line2", own_line, 2)
    scoped("cols_own", cols_own)
    for i in range(len(line)):
        scoped("extra_line%d" % i, extra_line, i)
    scoped("own_last", own_last)

    jobs = [("extra_relay", extra_relay)] if has_line else []
    jobs += [("cols_side", cols_side)]
    jobs += [("cols_line%d" % i, functools.partial(cols_line, i)) for i in range(len(line[:2]))]
    late = [("hidden%d" % k, functools.partial(hidden_piece, k)) for k in range(len(pieces))]
    group = n_t * depth
    for n, kind in enumerate(kinds):
        if n == 1:
            for job in jobs:
                scoped(*job)
            scoped("extra_last", extra_last)
            jobs = late
        blocks = cols_ref if n == 0 else extra
        for k, owner in enumerate((core, 1 - core)):
            left[pl.ds(k * group, group)] = (
                blocks[kind, owner].astype(jnp.float32).reshape(group, feats).astype(jnp.bfloat16)
            )
        for k, (start, width) in enumerate(spans):
            span = pl.ds(start, width)
            with jax.named_scope("w#n=%d" % n):
                weight_loads[n][k].wait()
            with jax.named_scope("dot#n=%d" % n):
                term = lax.dot_general(
                    left[...], weight[n, span], (((1,), (1,)), ((), ())), preferred_element_type=jnp.float32
                )
                if n > 0:
                    term = acc[:, span] + term
                if n < len(kinds) - 1:
                    acc[:, span] = term
                else:
                    grad_ref[:, span] = term[:group]
                    leave[:, span] = term[group:].astype(jnp.bfloat16)
            if n == len(kinds) - 1:
                send(leave.at[:, span], grad_sem.at[k], (mate, t), other_ref.at[:, span])
            if jobs:
                scoped(*jobs.pop(0))
    for job in jobs:
        scoped(*job)

    with jax.named_scope("tail_cols"):
        cols_last()
    with jax.named_scope("tail_hid"):
        for k, (start, width) in enumerate(pieces):
            for other in chips:
                arrived(hidden_ref.at[other, 1 - core, :, pl.ds(start, width)], hidden_sem.at[k, other, 1 - core])
        arrived(hidden_ref.at[chip, 1 - core], pair_sem.at[0])
    with jax.named_scope("tail_grad"):
        for k, (start, width) in enumerate(spans):
            arrived(other_ref.at[:, pl.ds(start, width)], grad_sem.at[k])
    with jax.named_scope("tail_send"):
        for copy in sent:
            copy.wait_send()


def finish_kernel(
    spans, cols_ref, hidden_ref, grad_ref, other_ref, act_ref, slope_ref,
    weight_out, gate_out, up_out, turned, gate, upper, weight_sem, grad_sem,
):
    copies = []
    for k, (start, width) in enumerate(spans):
        span = pl.ds(start, width)
        turned[span] = lax.dot_general(
            hidden_ref[:, span], cols_ref[...], (((0,), (0,)), ((), ())), preferred_element_type=jnp.float32
        )
        copies.append(pltpu.make_async_copy(turned.at[span], weight_out.at[span], weight_sem.at[k]))
        copies[-1].start()
        if k == 0:
            grad = grad_ref[...] + other_ref[...].astype(jnp.float32)
            upper[...] = (grad * act_ref[...]).astype(jnp.bfloat16)
            gate[...] = (grad * slope_ref[...]).astype(jnp.bfloat16)
            copies.append(pltpu.make_async_copy(upper, up_out, grad_sem.at[0]))
            copies.append(pltpu.make_async_copy(gate, gate_out, grad_sem.at[1]))
            copies[-2].start()
            copies[-1].start()
    for copy in copies:
        copy.wait()


def body(n_dp, n_t, grad_out, gate_pre, up_pre, down_weight):
    depth, model = grad_out.shape
    group, wide = gate_pre.shape
    feats = model // n_dp
    n_chip = n_dp // CORES
    outer = 4 if n_t % 4 == 0 else 1
    inner = n_t // outer
    spans = cut(wide, 512)
    pieces = cut(wide, 1024)
    n_line, n_side, n_other = outer - 1, inner - 1, n_chip - 1
    n_send = (
        n_other * CORES + n_chip * (CORES * (n_side + 2) + 1) + 2 * len(pieces) * n_other + 1
        + n_line * n_side + n_other * (n_line * n_side + 1 + 3 * n_side)
        + n_other * (n_side + 2 + 3 * n_side) + len(spans)
    )
    lanes = pl.cdiv(wide, 128) * 128
    results = 2 * n_dp * group * (feats + lanes) + (3 * 4 + 2) * group * lanes
    limit = VMEM - results - 64 * 1024
    anywhere = pl.BlockSpec(memory_space=pltpu.HBM)
    vmem = pl.BlockSpec(memory_space=pltpu.VMEM)
    dma = pltpu.SemaphoreType.DMA
    cols, hidden, *factors = pl.pallas_call(
        functools.partial(gather_kernel, n_dp, n_t, outer, spans, pieces),
        out_shape=[
            pltpu.VMEM((n_chip, CORES, n_t, depth, feats), jnp.bfloat16),
            pltpu.VMEM((n_chip, CORES, group, wide), jnp.bfloat16),
            pltpu.VMEM((group, wide), jnp.float32),
            pltpu.VMEM((group, wide), jnp.bfloat16),
            pltpu.VMEM((group, wide), jnp.float32),
            pltpu.VMEM((group, wide), jnp.float32),
        ],
        in_specs=[anywhere] * 4,
        out_specs=[vmem] * 6,
        scratch_shapes=[
            pltpu.VMEM((depth, model), jnp.bfloat16),
            pltpu.VMEM((n_chip, CORES, n_t, depth, feats), jnp.bfloat16),
            pltpu.VMEM((group, wide), jnp.bfloat16),
            pltpu.VMEM((group, wide), jnp.bfloat16),
            pltpu.VMEM((n_chip, wide, feats), jnp.bfloat16),
            pltpu.VMEM((CORES * group, feats), jnp.bfloat16),
            pltpu.VMEM((CORES * group, wide), jnp.float32),
            pltpu.VMEM((group, wide), jnp.bfloat16),
            dma((3,)),
            dma((n_chip, len(spans))),
            dma((n_send,)),
            dma((n_t,)),
            dma((n_chip, CORES, n_t)),
            dma((n_chip, CORES)),
            dma((2, n_chip, n_t)),
            dma((n_chip, inner)),
            dma((len(pieces), n_chip, CORES)),
            dma((1,)),
            dma((len(spans),)),
        ],
        compiler_params=pltpu.CompilerParams(collective_id=0, has_side_effects=True, vmem_limit_bytes=limit),
    )(grad_out, gate_pre, up_pre, down_weight.T)
    cols = cols.reshape(n_dp * group, feats)
    hidden = hidden.reshape(n_dp * group, wide)

    steps = [(0, min(128, wide))] + [(128 + start, width) for start, width in cut(wide - 128, 256)]
    turned, grad_gate, grad_up = pl.pallas_call(
        functools.partial(finish_kernel, steps),
        out_shape=[
            jax.ShapeDtypeStruct((wide, feats), jnp.float32),
            jax.ShapeDtypeStruct((group, wide), jnp.bfloat16),
            jax.ShapeDtypeStruct((group, wide), jnp.bfloat16),
        ],
        in_specs=[vmem] * 6,
        out_specs=[anywhere] * 3,
        scratch_shapes=[
            pltpu.VMEM((wide, feats), jnp.float32),
            pltpu.VMEM((group, wide), jnp.bfloat16),
            pltpu.VMEM((group, wide), jnp.bfloat16),
            dma((len(steps),)),
            dma((2,)),
        ],
        compiler_params=pltpu.CompilerParams(vmem_limit_bytes=limit),
    )(*[pltpu.with_memory_space_constraint(x, pltpu.VMEM) for x in (cols, hidden, *factors)])
    return turned.T, grad_gate, grad_up


def solution(mesh):
    in_specs = (P(("dp", "tensor"), None), P("dp", "tensor"), P("dp", "tensor"), P(None, "tensor"))
    out_specs = (P("dp", "tensor"), P("dp", "tensor"), P("dp", "tensor"))
    fn = functools.partial(body, mesh.shape["dp"], mesh.shape["tensor"])
    return jax.shard_map(fn, mesh=mesh, in_specs=in_specs, out_specs=out_specs, check_vma=False)
```

time: 30 us -> 25.6 us (0.85)
  Pallas kernels: 29.2 us -> 24.8 us
    pallas_call x2, Pallas kernels: 29.2 us -> 24.8 us  [the longest x1 21.3 us: body(): pl.pallas_call(functools.partial(gather_kernel, n_dp, n_t, outer, spans,...]
where the time goes in v1:
time: 25.6 us; the launch traced here: 25.5 us
  Pallas kernels  24.8 us (97%)
  between operations  0.64 us (2%)
    pallas_call x1, Pallas kernels, body(): pl.pallas_call(functools.partial(gather_kernel, n_dp, n_t, outer, spans,...  21.3 us
    pallas_call x1, Pallas kernels, body(): pl.pallas_call(functools.partial(finish_kernel, steps), out_shape=[jax.Sh...  3.55 us

profile of v1, /device:TPU:0, one launch (start us, length us, event | category | flops | bytes accessed | tf_op | source)
XLA Modules:
  0.0 25.5 jit_solution(9216663193876633213)
XLA Ops:
  0.6 21.3 %shard_map.67 = (bf16[2,2,8,8,1024]{4,3,2,1,0:T(8,128)(2,1)S(1)}, bf16[2,2,64,1856]{3,2,1,0:T(8,128)(2,1)S(1)}, f32[64,1856]{1,0:T(8,128)S(1)}, bf16[64,1856]{1,...) custom-call(bf16[8,4096]{1,0:T(8,128)(2,1)} %go_hbm.1, bf16[64,1856]{1,0:T(8,128)(2,1)} %gate_hbm.1, ...), custom_call_target="tpu_custom_call" | custom-call | tf_op jit(solution)/shard_map/pallas_call | solution.py:404
  21.9 3.5 %shard_map.68 = (f32[1856,1024]{1,0:T(8,128)}, bf16[64,1856]{1,0:T(8,128)(2,1)}, bf16[64,1856]{1,0:T(8,128)(2,1)}) custom-call(bf16[256,1024]{1,0:T(8,128)(2,1)S(1)} %bitcast.5, bf16[256,1856]{1,0:T(8,128)(2,1)S(1)} %bitcast.4, f32[64,1856]{1,0:T(8,128)S(1)} %get-tuple-element.14.grad_ref, bf16[64,1856]{1,0:T(8,128)(2,1)S(1)} %get-tuple-element.15.other_ref, ...), custom_call_target="tpu_custom_call" | custom-call | tf_op jit(solution)/shard_map/pallas_call | solution.py:443

commit v2 on v0

v2 whole, which is shorter than its diff:
```python
import functools

import jax
import jax.numpy as jnp
from jax import lax
from jax.experimental import pallas as pl
from jax.experimental.pallas import tpu as pltpu
from jax.sharding import PartitionSpec as P

MESH = pl.DeviceIdType.MESH
CORES = 2
VMEM = 67043328
MIDDLE, END = "middle", "end"
ORDER = (
    ("own", 0),
    ("own", 1, MIDDLE),
    ("cols",),
    ("extra", 0),
    ("extra", 1, MIDDLE),
    ("sides",),
    ("own", 2),
    ("own", 1, END),
    ("extra", 2),
    ("extra", 1, END),
    ("hidden", 0),
    ("owns",),
    ("dots", 0),
    ("hidden", 1),
    ("dots", 1),
    ("extras",),
)


def cut(wide, step):
    return [(start, min(step, wide - start)) for start in range(0, wide, step)]


def gather_kernel(
    n_dp, n_t, outer, spans, pieces,
    go_hbm, gate_hbm, up_hbm, weight_hbm,
    cols_ref, hidden_ref, grad_ref, other_ref, act_ref, slope_ref, extra, distant,
    mine, gate, upper, weight, left, leave, gauge,
    load_sem, weight_sem, send_sem, ready_sem, own_sem, extra_sem, cols_sem, hidden_sem,
):
    inner = n_t // outer
    n_chip = n_dp // CORES
    depth, feats = mine.shape[0], cols_ref.shape[-1]
    group = n_t * depth
    dp, t = lax.axis_index("dp"), lax.axis_index("tensor")
    chip, core = dp // CORES, dp % CORES
    mate = chip * CORES + (1 - core)
    a, b = t // inner, t % inner
    chips = [lax.rem(chip + d, n_chip) for d in range(1, n_chip)]
    sides = [lax.rem(b + d, inner) for d in range(1, inner)]
    n_other, n_side = len(chips), len(sides)

    has_line = outer == 4
    middle = (a * (3 - a)) // 2
    twin, mirror, across = a + 1 - 2 * (a % 2), 3 - a, (a + 2) % 4
    second = middle * mirror + (1 - middle) * across
    third = middle * across + (1 - middle) * mirror
    line = [twin, second, third] if has_line else []
    n_line = len(line)

    own_joint = own_sem.at[outer]
    cross, from_sides, late = (cols_sem.at[k] for k in range(3))

    def own_line_sem(step):
        return own_sem.at[step]

    def extra_line_sem(other, step):
        return extra_sem.at[other, step]

    def extra_joint(other):
        return extra_sem.at[other, outer]

    def at(step, side):
        return step * inner + side

    loads = [
        pltpu.make_async_copy(go_hbm, mine, load_sem.at[0]),
        pltpu.make_async_copy(gate_hbm, gate, load_sem.at[1]),
        pltpu.make_async_copy(up_hbm, upper, load_sem.at[2]),
    ]
    for load in loads:
        load.start()

    barrier = pltpu.get_barrier_semaphore()
    peers = [(lax.rem(dp + d, n_dp), t) for d in range(1, n_dp)]
    for c in range(CORES):
        peers += [(chip * CORES + c, at(a, side)) for side in sides]
        if has_line:
            peers.append((chip * CORES + c, at(twin, b)))
    for peer in peers:
        pl.semaphore_signal(barrier, inc=1, device_id=peer, device_id_type=MESH)
    if has_line:

        @pl.when(middle == 1)
        def _():
            for c in range(CORES):
                pl.semaphore_signal(barrier, inc=1, device_id=(chip * CORES + c, at(mirror, b)), device_id_type=MESH)

    with jax.named_scope("go"):
        loads[0].wait()
    with jax.named_scope("barrier"):
        pl.semaphore_wait(barrier, len(peers) + (CORES * middle if has_line else 0))

    if has_line:

        @pl.when(middle == 1)
        def _():
            pl.semaphore_signal(ready_sem.at[0], inc=1, device_id=(dp, at(mirror, b)), device_id_type=MESH)

    sent, sent_middle, sent_end = [], [], []

    def copy_to(block, sem, peer, dst=None, lane=0):
        return pltpu.make_async_remote_copy(
            src_ref=block, dst_ref=block if dst is None else dst, send_sem=send_sem.at[lane], recv_sem=sem,
            device_id=peer, device_id_type=MESH,
        )

    def arrived(blocks, sem):
        copy_to(gauge.at[pl.ds(0, blocks)], sem, (mate, t)).wait_recv()

    def block_of(group):
        return pl.ds(pl.multiple_of(group * feats, feats), feats)

    def blocks_in(block):
        size = 1
        for dim in block.shape:
            size *= dim
        return size // (depth * feats)

    def send(block, sem, peer, dst=None):
        sent.append(blocks_in(block))
        copy_to(block, sem, peer, dst).start()

    def send_middle(block, sem, peer, dst=None):
        sent_middle.append(blocks_in(block))

        @pl.when(middle == 1)
        def _():
            copy_to(block, sem, peer, dst).start()

    for other in chips:
        for c in range(CORES):
            group_of = other * CORES + c
            send(mine.at[:, block_of(group_of)], cross, (group_of, t), cols_ref.at[chip, core, t])

    def send_end(block, sem, peer, dst=None):
        sent_end.append(blocks_in(block))

        @pl.when(middle == 0)
        def _():
            copy_to(block, sem, peer, dst).start()

    def pair_of(other):
        return pl.ds(pl.multiple_of(other * CORES * feats, CORES * feats), CORES * feats)

    def own_block(source, dst, line_sem, joint):
        for c in range(CORES):
            target = chip * CORES + c
            block = mine.at[:, block_of(source * CORES + c)]
            for side in sides:
                send(block, joint, (target, at(a, side)), dst)
            if has_line:
                send(block, line_sem, (target, at(twin, b)), dst)
                send_middle(block, line_sem, (target, at(mirror, b)), dst)
        send(mine.at[:, block_of(source * CORES + 1 - core)], joint, (mate, t), dst)

    own_block(chip, cols_ref.at[chip, core, t], own_line_sem(a), own_joint)
    for n, other in enumerate(chips):
        block = mine.at[:, pair_of(other)]
        for side in sides:
            send(block, extra_joint(n), (dp, at(a, side)), extra.at[n, t])
        if has_line:
            send(block, extra_line_sem(n, a), (dp, at(twin, b)), extra.at[n, t])
            send_middle(block, extra_line_sem(n, a), (dp, at(mirror, b)), extra.at[n, t])

    def own_far():
        @pl.when(middle == 1)
        def _():
            pl.semaphore_wait(ready_sem.at[0], 1)
            pl.semaphore_signal(ready_sem.at[1], inc=1, device_id=(dp, at(twin, b)), device_id_type=MESH)

        @pl.when(middle == 0)
        def _():
            pl.semaphore_wait(ready_sem.at[1], 1)

        for c in range(CORES):
            block = mine.at[:, block_of(chip * CORES + c)]
            send_end(block, own_line_sem(a), (chip * CORES + c, at(mirror, b)), cols_ref.at[chip, core, t])
        for n, other in enumerate(chips):
            send_end(mine.at[:, pair_of(other)], extra_line_sem(n, a), (dp, at(mirror, b)), extra.at[n, t])

    with jax.named_scope("hid_load"):
        loads[1].wait()
        loads[2].wait()
    weight_loads = [
        pltpu.make_async_copy(
            weight_hbm.at[pl.ds(start, width), block_of(dp)], weight.at[pl.ds(start, width)], weight_sem.at[k],
        )
        for k, (start, width) in enumerate(spans)
    ]
    weight_loads += [
        pltpu.make_async_copy(weight_hbm.at[:, pair_of(other)], distant.at[n], weight_sem.at[len(spans) + n])
        for n, other in enumerate(chips)
    ]
    with jax.named_scope("hid"):
        g = gate[...].astype(jnp.float32)
        u = upper[...].astype(jnp.float32)
        sig = jax.nn.sigmoid(g)
        hidden_ref[chip, core] = (g * sig * u).astype(jnp.bfloat16)
        act_ref[...] = g * sig
        slope_ref[...] = u * sig * (1.0 + g * (1.0 - sig))
    hidden_mate, grad_mate = hidden_sem.at[len(pieces)], hidden_sem.at[len(pieces) + 1]
    for k, (start, width) in enumerate(pieces):
        piece = hidden_ref.at[chip, core, :, pl.ds(start, width)]
        for other in chips:
            copy_to(piece, hidden_sem.at[k], (other * CORES + core, t), lane=1).start()
    copy_to(hidden_ref.at[chip, core], hidden_mate, (mate, t), lane=1).start()
    for load in weight_loads:
        load.start()
    if has_line:
        with jax.named_scope("own_far"):
            own_far()
    cols_ref[chip, core, t] = mine[:, block_of(dp)]
    for n, other in enumerate(chips):
        extra[n, t] = mine[:, pair_of(other)]

    def onward(i):
        return (dp, at(mirror if i == 0 else twin, b))

    def only(job):
        counted = set()

        def run(*args, where=None):
            kept = list(sent), list(sent_middle), list(sent_end)
            if where is None:
                job(*args)
            else:
                pl.when(middle == where)(functools.partial(job, *args))
            if args in counted:
                sent[:], sent_middle[:], sent_end[:] = kept
            counted.add(args)

        return run

    @only
    def own_line(i):
        block, sem = cols_ref.at[chip, :, at(line[i], b)], own_line_sem(line[i])
        arrived(CORES, sem)
        if i < 2:
            send_middle(block, sem, onward(i))
        for side in sides:
            send(block, own_joint, (dp, at(a, side)))

    @only
    def extra_line(i):
        source = at(line[i], b)
        for n, other in enumerate(chips):
            block, sem = extra.at[n, source], extra_line_sem(n, line[i])
            arrived(CORES, sem)
            if i < 2:
                send_middle(block, sem, onward(i))
            for side in sides:
                send(block, extra_joint(n), (dp, at(a, side)))
            if i == 2:
                for c in range(CORES):
                    block = extra.at[n, source, :, pl.ds(c * feats, feats)]
                    for side in [b] + sides:
                        send(block, late, (other * CORES + c, at(a, side)), cols_ref.at[chip, core, source])

    @only
    def own_last():
        arrived(n_side * (1 + n_line) * CORES + 1, own_joint)

    @only
    def extra_last():
        for n in range(n_other):
            arrived(n_side * (1 + n_line) * CORES, extra_joint(n))

    def cols_along(side):
        for other in chips:
            block = cols_ref.at[other, :, at(a, side)]
            send(block, late, (dp, at(twin, b)))
            send_middle(block, late, (dp, at(mirror, b)))
            send_middle(block, late, (dp, at(across, b)))

    @only
    def cols_own():
        arrived(n_other * CORES, cross)
        for other in chips:
            for side in sides:
                send(cols_ref.at[other, :, t], from_sides, (dp, at(a, side)))
        if has_line:
            cols_along(b)

    @only
    def cols_sides():
        if n_side:
            arrived(n_other * n_side * CORES, from_sides)
        if has_line:
            for side in sides:
                cols_along(side)

    def cols_last():
        if has_line:
            arrived(3 * n_other * (1 + n_side) * CORES, late)

    @only
    def hidden_piece(k):
        start, width = pieces[k]
        for other in chips:
            piece = hidden_ref.at[other, core, :, pl.ds(start, width)]
            copy_to(piece, hidden_sem.at[k], (mate, t), lane=1).wait_recv()
        for other in chips:
            piece = hidden_ref.at[other, core, :, pl.ds(start, width)]
            copy_to(piece, hidden_mate, (mate, t), lane=1).start()

    def scoped(name, job, *args):
        with jax.named_scope(name):
            return job(*args)

    def dot(k):
        if k >= len(spans):
            return
        if k == 0:
            for place, owner in enumerate((core, 1 - core)):
                left[pl.ds(place * group, group)] = (
                    cols_ref[chip, owner].astype(jnp.float32).reshape(group, feats).astype(jnp.bfloat16)
                )
        start, width = spans[k]
        span = pl.ds(start, width)
        weight_loads[k].wait()
        term = lax.dot_general(
            left[...], weight[span], (((1,), (1,)), ((), ())), preferred_element_type=jnp.float32
        )
        grad_ref[:, span] = term[:group]
        leave[:, span] = term[group:].astype(jnp.bfloat16)
        copy_to(leave.at[:, span], grad_mate, (mate, t), other_ref.at[:, span], 1).start()

    jobs = {
        "own": own_line, "extra": extra_line, "cols": cols_own, "sides": cols_sides,
        "owns": own_last, "extras": extra_last, "hidden": hidden_piece, "dots": dot,
    }
    line_jobs = ("own", "extra")
    for name, *rest in ORDER:
        if name in line_jobs and not has_line or name == "hidden" and rest[0] >= len(pieces):
            continue
        where = rest.pop() if rest and rest[-1] in (MIDDLE, END) else None
        if where is None:
            scoped(name + "".join(map(str, rest)), jobs[name], *rest)
        else:
            scoped(name + "".join(map(str, rest)) + where[0], functools.partial(jobs[name], where=int(where == MIDDLE)), *rest)

    for load in weight_loads[len(spans):]:
        load.wait()
    with jax.named_scope("tail_cols"):
        cols_last()
    with jax.named_scope("tail_hid"):
        everyone = hidden_ref.at[:, 1 - core]
        copy_to(everyone, hidden_mate, (mate, t), lane=1).wait_recv()
    with jax.named_scope("tail_grad"):
        copy_to(leave, grad_mate, (mate, t), other_ref, 1).wait_recv()
    with jax.named_scope("tail_send"):
        copy_to(gauge.at[pl.ds(0, sum(sent))], late, (mate, t)).wait_send()
        if has_line:

            @pl.when(middle == 1)
            def _():
                copy_to(gauge.at[pl.ds(0, sum(sent_middle))], late, (mate, t)).wait_send()

            @pl.when(middle == 0)
            def _():
                copy_to(gauge.at[pl.ds(0, sum(sent_end))], late, (mate, t)).wait_send()

        copy_to(hidden_ref, hidden_mate, (mate, t), lane=1).wait_send()


def finish_kernel(
    spans, chunks, cols_ref, hidden_ref, grad_ref, other_ref, act_ref, slope_ref, extra_ref, distant_ref,
    weight_out, gate_out, up_out, turned, gate, upper, left, weight_sem, grad_sem,
):
    copies = []

    def leave(src, dst, sem):
        copies.append(pltpu.make_async_copy(src, dst, sem))
        copies[-1].start()

    for k, (start, width) in enumerate(spans):
        span = pl.ds(start, width)
        turned[span] = lax.dot_general(
            hidden_ref[:, span], cols_ref[...], (((0,), (0,)), ((), ())), preferred_element_type=jnp.float32
        )
        leave(turned.at[span], weight_out.at[span], weight_sem.at[k])
    n_other, _, _, pair = extra_ref.shape
    for n in range(n_other):
        left[n] = extra_ref[n].astype(jnp.float32).reshape(left.shape[1], pair).astype(jnp.bfloat16)
    for k, (start, width) in enumerate(chunks):
        span = pl.ds(start, width)
        grad = grad_ref[:, span] + other_ref[:, span].astype(jnp.float32)
        for n in range(n_other):
            grad += lax.dot_general(
                left[n], distant_ref[n, span], (((1,), (1,)), ((), ())), preferred_element_type=jnp.float32
            )
        upper[:, span] = (grad * act_ref[:, span]).astype(jnp.bfloat16)
        gate[:, span] = (grad * slope_ref[:, span]).astype(jnp.bfloat16)
    leave(upper, up_out, grad_sem.at[0])
    leave(gate, gate_out, grad_sem.at[1])
    for copy in copies:
        copy.wait()


def body(n_dp, n_t, grad_out, gate_pre, up_pre, down_weight):
    depth, model = grad_out.shape
    group, wide = gate_pre.shape
    feats = model // n_dp
    n_chip = n_dp // CORES
    outer = 4 if n_t % 4 == 0 else 1
    inner = n_t // outer
    spans = cut(wide, 1024)
    pieces = cut(wide, 1024)
    n_side, n_other = inner - 1, n_chip - 1
    n_gauge = (n_chip + 1) * (n_side + 4) * 2 + 3 * n_side * 2 + n_other * (16 * n_side + 12)
    lanes = pl.cdiv(wide, 128) * 128
    pair = CORES * feats
    results = 2 * (n_dp * group * (feats + lanes) + 7 * group * lanes + n_other * (group + wide) * pair)
    limit = VMEM - results - 64 * 1024
    anywhere = pl.BlockSpec(memory_space=pltpu.HBM)
    vmem = pl.BlockSpec(memory_space=pltpu.VMEM)
    dma = pltpu.SemaphoreType.DMA
    cols, hidden, *factors = pl.pallas_call(
        functools.partial(gather_kernel, n_dp, n_t, outer, spans, pieces),
        out_shape=[
            pltpu.VMEM((n_chip, CORES, n_t, depth, feats), jnp.bfloat16),
            pltpu.VMEM((n_chip, CORES, group, wide), jnp.bfloat16),
            pltpu.VMEM((group, wide), jnp.float32),
            pltpu.VMEM((group, wide), jnp.bfloat16),
            pltpu.VMEM((group, wide), jnp.float32),
            pltpu.VMEM((group, wide), jnp.float32),
            pltpu.VMEM((n_other, n_t, depth, pair), jnp.bfloat16),
            pltpu.VMEM((n_other, wide, pair), jnp.bfloat16),
        ],
        in_specs=[anywhere] * 4,
        out_specs=[vmem] * 8,
        scratch_shapes=[
            pltpu.VMEM((depth, model), jnp.bfloat16),
            pltpu.VMEM((group, wide), jnp.bfloat16),
            pltpu.VMEM((group, wide), jnp.bfloat16),
            pltpu.VMEM((wide, feats), jnp.bfloat16),
            pltpu.VMEM((CORES * group, feats), jnp.bfloat16),
            pltpu.VMEM((group, wide), jnp.bfloat16),
            pltpu.VMEM((n_gauge, depth, feats), jnp.bfloat16),
            dma((3,)),
            dma((len(spans) + n_other,)),
            dma((2,)),
            pltpu.SemaphoreType.REGULAR((2,)),
            dma((outer + 1,)),
            dma((n_other, outer + 1)),
            dma((3,)),
            dma((len(pieces) + 2,)),
        ],
        compiler_params=pltpu.CompilerParams(collective_id=0, has_side_effects=True, vmem_limit_bytes=limit),
    )(grad_out, gate_pre, up_pre, down_weight.T)
    cols = cols.reshape(n_dp * group, feats)
    hidden = hidden.reshape(n_dp * group, wide)

    steps = [(0, min(128, wide))] + [(128 + start, width) for start, width in cut(wide - 128, 256)]
    turned, grad_gate, grad_up = pl.pallas_call(
        functools.partial(finish_kernel, steps, cut(wide, 512)),
        out_shape=[
            jax.ShapeDtypeStruct((wide, feats), jnp.float32),
            jax.ShapeDtypeStruct((group, wide), jnp.bfloat16),
            jax.ShapeDtypeStruct((group, wide), jnp.bfloat16),
        ],
        in_specs=[vmem] * 8,
        out_specs=[anywhere] * 3,
        scratch_shapes=[
            pltpu.VMEM((wide, feats), jnp.float32),
            pltpu.VMEM((group, wide), jnp.bfloat16),
            pltpu.VMEM((group, wide), jnp.bfloat16),
            pltpu.VMEM((n_other, group, pair), jnp.bfloat16),
            dma((len(steps),)),
            dma((2,)),
        ],
        compiler_params=pltpu.CompilerParams(vmem_limit_bytes=limit),
    )(*[pltpu.with_memory_space_constraint(x, pltpu.VMEM) for x in (cols, hidden, *factors)])
    return turned.T, grad_gate, grad_up


def solution(mesh):
    in_specs = (P(("dp", "tensor"), None), P("dp", "tensor"), P("dp", "tensor"), P(None, "tensor"))
    out_specs = (P("dp", "tensor"), P("dp", "tensor"), P("dp", "tensor"))
    fn = functools.partial(body, mesh.shape["dp"], mesh.shape["tensor"])
    return jax.shard_map(fn, mesh=mesh, in_specs=in_specs, out_specs=out_specs, check_vma=False)
```

time: 30 us -> 22.9 us (0.76)
  Pallas kernels: 29.2 us -> 22.1 us
    pallas_call x2, Pallas kernels: 29.2 us -> 22.1 us  [the longest x1 17.7 us: body(): pl.pallas_call(functools.partial(gather_kernel, n_dp, n_t, outer, spans,...]
where the time goes in v2:
time: 22.9 us; the launch traced here: 22.8 us
  Pallas kernels  22.1 us (97%)
  between operations  0.64 us (3%)
    pallas_call x1, Pallas kernels, body(): pl.pallas_call(functools.partial(gather_kernel, n_dp, n_t, outer, spans,...  17.7 us
    pallas_call x1, Pallas kernels, body(): pl.pallas_call(functools.partial(finish_kernel, steps, cut(wide, 512)), o...  4.42 us

profile of v2, /device:TPU:0, one launch (start us, length us, event | category | flops | bytes accessed | tf_op | source)
XLA Modules:
  0.0 22.8 jit_solution(5638870313847763160)
XLA Ops:
  0.6 17.7 %shard_map.67 = (bf16[2,2,8,8,1024]{4,3,2,1,0:T(8,128)(2,1)S(1)}, bf16[2,2,64,1856]{3,2,1,0:T(8,128)(2,1)S(1)}, f32[64,1856]{1,0:T(8,128)S(1)}, bf16[64,1856]{1,...) custom-call(bf16[8,4096]{1,0:T(8,128)(2,1)} %go_hbm.1, ...), custom_call_target="tpu_custom_call" | custom-call | tf_op jit(solution)/shard_map/pallas_call | solution.py:433
  18.4 4.4 %shard_map.68 = (f32[1856,1024]{1,0:T(8,128)}, bf16[64,1856]{1,0:T(8,128)(2,1)}, bf16[64,1856]{1,0:T(8,128)(2,1)}) custom-call(bf16[256,1024]{1,0:T(8,128)(2,1)S(1)} %bitcast.5, bf16[256,1856]{1,0:T(8,128)(2,1)S(1)} %bitcast.4, f32[64,1856]{1,0:T(8,128)S(1)} %get-tuple-element.16.grad_ref, bf16[64,1856]{1,0:T(8,128)(2,1)S(1)} %get-tuple-element.17.other_ref, ...), custom_call_target="tpu_custom_call" | custom-call | tf_op jit(solution)/shard_map/pallas_call | solution.py:470

commit v3 on v2

--- a/solution.py
+++ b/solution.py
@@ -10,6 +10,8 @@
 MESH = pl.DeviceIdType.MESH
 CORES = 2
 VMEM = 67043328
+SLICE = 512
+TURNS = 4
 MIDDLE, END = "middle", "end"
 ORDER = (
     ("own", 0),
@@ -17,10 +19,15 @@
     ("cols",),
     ("extra", 0),
     ("extra", 1, MIDDLE),
+    ("turn", 0),
+    ("turn", 1),
+    ("turn", 2),
+    ("turn", 3),
     ("sides",),
     ("own", 2),
     ("own", 1, END),
     ("extra", 2),
+    ("turn", 4),
     ("extra", 1, END),
     ("hidden", 0),
     ("owns",),
@@ -39,7 +46,7 @@
     n_dp, n_t, outer, spans, pieces,
     go_hbm, gate_hbm, up_hbm, weight_hbm,
     cols_ref, hidden_ref, grad_ref, other_ref, act_ref, slope_ref, extra, distant,
-    mine, gate, upper, weight, left, leave, gauge,
+    mine, gate, upper, weight, flat, plain, left, leave, gauge,
     load_sem, weight_sem, send_sem, ready_sem, own_sem, extra_sem, cols_sem, hidden_sem,
 ):
     inner = n_t // outer
@@ -196,15 +203,17 @@
     with jax.named_scope("hid_load"):
         loads[1].wait()
         loads[2].wait()
+    slices = [
+        (plain.at[n], distant.at[n], other * CORES * feats, start, width)
+        for n, other in enumerate(chips) for start, width in cut(CORES * feats, SLICE)
+    ]
+    slices += [(flat, weight, dp * feats, start, width) for start, width in cut(feats, SLICE)]
+    n_own = len(cut(feats, SLICE))
     weight_loads = [
         pltpu.make_async_copy(
-            weight_hbm.at[pl.ds(start, width), block_of(dp)], weight.at[pl.ds(start, width)], weight_sem.at[k],
+            weight_hbm.at[:, pl.ds(pl.multiple_of(first + start, width), width)], raw.at[:, pl.ds(start, width)], weight_sem.at[k],
         )
-        for k, (start, width) in enumerate(spans)
-    ]
-    weight_loads += [
-        pltpu.make_async_copy(weight_hbm.at[:, pair_of(other)], distant.at[n], weight_sem.at[len(spans) + n])
-        for n, other in enumerate(chips)
+        for k, (raw, _, first, start, width) in enumerate(slices)
     ]
     with jax.named_scope("hid"):
         g = gate[...].astype(jnp.float32)
@@ -332,17 +341,24 @@
                 )
         start, width = spans[k]
         span = pl.ds(start, width)
-        weight_loads[k].wait()
         term = lax.dot_general(
-            left[...], weight[span], (((1,), (1,)), ((), ())), preferred_element_type=jnp.float32
+            left[...], weight[:, span], (((1,), (0,)), ((), ())), preferred_element_type=jnp.float32
         )
         grad_ref[:, span] = term[:group]
         leave[:, span] = term[group:].astype(jnp.bfloat16)
         copy_to(leave.at[:, span], grad_mate, (mate, t), other_ref.at[:, span], 1).start()
 
+    def turn(q):
+        for k, (raw, turned, _, start, width) in enumerate(slices):
+            far = len(slices) - n_own
+            if (k * TURNS // far if k < far else TURNS) == q:
+                weight_loads[k].wait()
+                span = pl.ds(start, width)
+                turned[span] = raw[:, span].T
+
     jobs = {
         "own": own_line, "extra": extra_line, "cols": cols_own, "sides": cols_sides,
-        "owns": own_last, "extras": extra_last, "hidden": hidden_piece, "dots": dot,
+        "owns": own_last, "extras": extra_last, "hidden": hidden_piece, "dots": dot, "turn": turn,
     }
     line_jobs = ("own", "extra")
     for name, *rest in ORDER:
@@ -354,8 +370,6 @@
         else:
             scoped(name + "".join(map(str, rest)) + where[0], functools.partial(jobs[name], where=int(where == MIDDLE)), *rest)
 
-    for load in weight_loads[len(spans):]:
-        load.wait()
     with jax.named_scope("tail_cols"):
         cols_last()
     with jax.named_scope("tail_hid"):
@@ -401,9 +415,7 @@
         span = pl.ds(start, width)
         grad = grad_ref[:, span] + other_ref[:, span].astype(jnp.float32)
         for n in range(n_other):
-            grad += lax.dot_general(
-                left[n], distant_ref[n, span], (((1,), (1,)), ((), ())), preferred_element_type=jnp.float32
-            )
+            grad += jnp.dot(left[n], distant_ref[n, :, span], preferred_element_type=jnp.float32)
         upper[:, span] = (grad * act_ref[:, span]).astype(jnp.bfloat16)
         gate[:, span] = (grad * slope_ref[:, span]).astype(jnp.bfloat16)
     leave(upper, up_out, grad_sem.at[0])
@@ -425,7 +437,7 @@
     n_gauge = (n_chip + 1) * (n_side + 4) * 2 + 3 * n_side * 2 + n_other * (16 * n_side + 12)
     lanes = pl.cdiv(wide, 128) * 128
     pair = CORES * feats
-    results = 2 * (n_dp * group * (feats + lanes) + 7 * group * lanes + n_other * (group + wide) * pair)
+    results = 2 * (n_dp * group * (feats + lanes) + 7 * group * lanes + n_other * (group + lanes) * pair)
     limit = VMEM - results - 64 * 1024
     anywhere = pl.BlockSpec(memory_space=pltpu.HBM)
     vmem = pl.BlockSpec(memory_space=pltpu.VMEM)
@@ -440,7 +452,7 @@
             pltpu.VMEM((group, wide), jnp.float32),
             pltpu.VMEM((group, wide), jnp.float32),
             pltpu.VMEM((n_other, n_t, depth, pair), jnp.bfloat16),
-            pltpu.VMEM((n_other, wide, pair), jnp.bfloat16),
+            pltpu.VMEM((n_other, pair, wide), jnp.bfloat16),
         ],
         in_specs=[anywhere] * 4,
         out_specs=[vmem] * 8,
@@ -448,12 +460,14 @@
             pltpu.VMEM((depth, model), jnp.bfloat16),
             pltpu.VMEM((group, wide), jnp.bfloat16),
             pltpu.VMEM((group, wide), jnp.bfloat16),
+            pltpu.VMEM((feats, wide), jnp.bfloat16),
             pltpu.VMEM((wide, feats), jnp.bfloat16),
+            pltpu.VMEM((n_other, wide, pair), jnp.bfloat16),
             pltpu.VMEM((CORES * group, feats), jnp.bfloat16),
             pltpu.VMEM((group, wide), jnp.bfloat16),
             pltpu.VMEM((n_gauge, depth, feats), jnp.bfloat16),
             dma((3,)),
-            dma((len(spans) + n_other,)),
+            dma((n_other * len(cut(pair, SLICE)) + len(cut(feats, SLICE)),)),
             dma((2,)),
             pltpu.SemaphoreType.REGULAR((2,)),
             dma((outer + 1,)),

time: 22.9 us -> 21.5 us (0.939)
  Pallas kernels: 22.1 us -> 20.7 us
    pallas_call x1, Pallas kernels: 4.42 us -> 3.64 us  [body(): pl.pallas_call(functools.partial(finish_kernel, steps, cut(wide, 512)), o...]
    pallas_call x1, Pallas kernels: 17.7 us -> 17 us  [body(): pl.pallas_call(functools.partial(gather_kernel, n_dp, n_t, outer, spans,...]
where the time goes in v3:
time: 21.5 us; the launch traced here: 21.3 us
  Pallas kernels  20.7 us (96%)
  between operations  0.64 us (3%)
    pallas_call x1, Pallas kernels, body(): pl.pallas_call(functools.partial(gather_kernel, n_dp, n_t, outer, spans,...  17 us
    pallas_call x1, Pallas kernels, body(): pl.pallas_call(functools.partial(finish_kernel, steps, cut(wide, 512)), o...  3.64 us

profile of v3, /device:TPU:0, one launch (start us, length us, event | category | flops | bytes accessed | tf_op | source)
XLA Modules:
  0.0 21.3 jit_solution(13752748247583993979)
XLA Ops:
  0.6 17.0 %shard_map.67 = (bf16[2,2,8,8,1024]{4,3,2,1,0:T(8,128)(2,1)S(1)}, bf16[2,2,64,1856]{3,2,1,0:T(8,128)(2,1)S(1)}, f32[64,1856]{1,0:T(8,128)S(1)}, bf16[64,1856]{1,...) custom-call(bf16[8,4096]{1,0:T(8,128)(2,1)} %go_hbm.1, ...), custom_call_target="tpu_custom_call" | custom-call | tf_op jit(solution)/shard_map/pallas_call | solution.py:445
  17.7 3.6 %shard_map.68 = (f32[1856,1024]{1,0:T(8,128)}, bf16[64,1856]{1,0:T(8,128)(2,1)}, bf16[64,1856]{1,0:T(8,128)(2,1)}) custom-call(bf16[256,1024]{1,0:T(8,128)(2,1)S(1)} %bitcast.5, bf16[256,1856]{1,0:T(8,128)(2,1)S(1)} %bitcast.4, f32[64,1856]{1,0:T(8,128)S(1)} %get-tuple-element.16.grad_ref, bf16[64,1856]{1,0:T(8,128)(2,1)S(1)} %get-tuple-element.17.other_ref, ...), custom_call_target="tpu_custom_call" | custom-call | tf_op jit(solution)/shard_map/pallas_call | solution.py:484

commit v4 on v3

--- a/solution.py
+++ b/solution.py
@@ -21,14 +21,15 @@
     ("extra", 1, MIDDLE),
     ("turn", 0),
     ("turn", 1),
+    ("own", 1, END),
+    ("own", 2),
     ("turn", 2),
     ("turn", 3),
+    ("extra", 1, END),
     ("sides",),
-    ("own", 2),
-    ("own", 1, END),
     ("extra", 2),
+    ("far",),
     ("turn", 4),
-    ("extra", 1, END),
     ("hidden", 0),
     ("owns",),
     ("dots", 0),
@@ -197,8 +198,11 @@
         for c in range(CORES):
             block = mine.at[:, block_of(chip * CORES + c)]
             send_end(block, own_line_sem(a), (chip * CORES + c, at(mirror, b)), cols_ref.at[chip, core, t])
+            send_middle(block, own_line_sem(a), (chip * CORES + c, at(across, b)), cols_ref.at[chip, core, t])
         for n, other in enumerate(chips):
-            send_end(mine.at[:, pair_of(other)], extra_line_sem(n, a), (dp, at(mirror, b)), extra.at[n, t])
+            block = mine.at[:, pair_of(other)]
+            send_end(block, extra_line_sem(n, a), (dp, at(mirror, b)), extra.at[n, t])
+            send_middle(block, extra_line_sem(n, a), (dp, at(across, b)), extra.at[n, t])
 
     with jax.named_scope("hid_load"):
         loads[1].wait()
@@ -237,9 +241,6 @@
     for n, other in enumerate(chips):
         extra[n, t] = mine[:, pair_of(other)]
 
-    def onward(i):
-        return (dp, at(mirror if i == 0 else twin, b))
-
     def only(job):
         counted = set()
 
@@ -259,8 +260,8 @@
     def own_line(i):
         block, sem = cols_ref.at[chip, :, at(line[i], b)], own_line_sem(line[i])
         arrived(CORES, sem)
-        if i < 2:
-            send_middle(block, sem, onward(i))
+        if i == 0:
+            send_middle(block, sem, (dp, at(mirror, b)))
         for side in sides:
             send(block, own_joint, (dp, at(a, side)))
 
@@ -270,15 +271,18 @@
         for n, other in enumerate(chips):
             block, sem = extra.at[n, source], extra_line_sem(n, line[i])
             arrived(CORES, sem)
-            if i < 2:
-                send_middle(block, sem, onward(i))
+            if i == 0:
+                send_middle(block, sem, (dp, at(mirror, b)))
             for side in sides:
                 send(block, extra_joint(n), (dp, at(a, side)))
-            if i == 2:
-                for c in range(CORES):
-                    block = extra.at[n, source, :, pl.ds(c * feats, feats)]
-                    for side in [b] + sides:
-                        send(block, late, (other * CORES + c, at(a, side)), cols_ref.at[chip, core, source])
+
+    def extra_far():
+        source = at(third, b)
+        for n, other in enumerate(chips):
+            for c in range(CORES):
+                block = extra.at[n, source, :, pl.ds(c * feats, feats)]
+                for side in [b] + sides:
+                    send(block, late, (other * CORES + c, at(a, side)), cols_ref.at[chip, core, source])
 
     @only
     def own_last():
@@ -358,9 +362,9 @@
 
     jobs = {
         "own": own_line, "extra": extra_line, "cols": cols_own, "sides": cols_sides,
-        "owns": own_last, "extras": extra_last, "hidden": hidden_piece, "dots": dot, "turn": turn,
+        "owns": own_last, "extras": extra_last, "hidden": hidden_piece, "dots": dot, "turn": turn, "far": extra_far,
     }
-    line_jobs = ("own", "extra")
+    line_jobs = ("own", "extra", "far")
     for name, *rest in ORDER:
         if name in line_jobs and not has_line or name == "hidden" and rest[0] >= len(pieces):
             continue

time: 21.5 us -> 21.2 us (0.986)
  Pallas kernels: 20.7 us -> 20.4 us
    pallas_call x1, Pallas kernels: 17 us -> 16.8 us  [body(): pl.pallas_call(functools.partial(gather_kernel, n_dp, n_t, outer, spans,...]
where the time goes in v4:
time: 21.2 us; the launch traced here: 21.1 us
  Pallas kernels  20.4 us (96%)
  between operations  0.64 us (3%)
    pallas_call x1, Pallas kernels, body(): pl.pallas_call(functools.partial(gather_kernel, n_dp, n_t, outer, spans,...  16.8 us
    pallas_call x1, Pallas kernels, body(): pl.pallas_call(functools.partial(finish_kernel, steps, cut(wide, 512)), o...  3.63 us

profile of v4, /device:TPU:0, one launch (start us, length us, event | category | flops | bytes accessed | tf_op | source)
XLA Modules:
  0.0 21.1 jit_solution(296297926281938861)
XLA Ops:
  0.6 16.8 %shard_map.67 = (bf16[2,2,8,8,1024]{4,3,2,1,0:T(8,128)(2,1)S(1)}, bf16[2,2,64,1856]{3,2,1,0:T(8,128)(2,1)S(1)}, f32[64,1856]{1,0:T(8,128)S(1)}, bf16[64,1856]{1,...) custom-call(bf16[8,4096]{1,0:T(8,128)(2,1)} %go_hbm.1, ...), custom_call_target="tpu_custom_call" | custom-call | tf_op jit(solution)/shard_map/pallas_call | solution.py:449
  17.4 3.6 %shard_map.68 = (f32[1856,1024]{1,0:T(8,128)}, bf16[64,1856]{1,0:T(8,128)(2,1)}, bf16[64,1856]{1,0:T(8,128)(2,1)}) custom-call(bf16[256,1024]{1,0:T(8,128)(2,1)S(1)} %bitcast.5, bf16[256,1856]{1,0:T(8,128)(2,1)S(1)} %bitcast.4, f32[64,1856]{1,0:T(8,128)S(1)} %get-tuple-element.16.grad_ref, bf16[64,1856]{1,0:T(8,128)(2,1)S(1)} %get-tuple-element.17.other_ref, ...), custom_call_target="tpu_custom_call" | custom-call | tf_op jit(solution)/shard_map/pallas_call | solution.py:488

commit v5 on v4

--- a/solution.py
+++ b/solution.py
@@ -23,10 +23,8 @@
     ("turn", 1),
     ("own", 1, END),
     ("own", 2),
-    ("turn", 2),
-    ("turn", 3),
+    ("sides",),
     ("extra", 1, END),
-    ("sides",),
     ("extra", 2),
     ("far",),
     ("turn", 4),
@@ -35,6 +33,8 @@
     ("dots", 0),
     ("hidden", 1),
     ("dots", 1),
+    ("turn", 2),
+    ("turn", 3),
     ("extras",),
 )
 

time: 21.2 us -> 21.2 us (level)
  no operation moved by 1% of the time
where the time goes in v5:
time: 21.2 us; the launch traced here: 21.1 us
  Pallas kernels  20.4 us (96%)
  between operations  0.64 us (3%)
    pallas_call x1, Pallas kernels, body(): pl.pallas_call(functools.partial(gather_kernel, n_dp, n_t, outer, spans,...  16.8 us
    pallas_call x1, Pallas kernels, body(): pl.pallas_call(functools.partial(finish_kernel, steps, cut(wide, 512)), o...  3.63 us

profile of v5, /device:TPU:0, one launch (start us, length us, event | category | flops | bytes accessed | tf_op | source)
XLA Modules:
  0.0 21.1 jit_solution(7526662669757376386)
XLA Ops:
  0.6 16.8 %shard_map.67 = (bf16[2,2,8,8,1024]{4,3,2,1,0:T(8,128)(2,1)S(1)}, bf16[2,2,64,1856]{3,2,1,0:T(8,128)(2,1)S(1)}, f32[64,1856]{1,0:T(8,128)S(1)}, bf16[64,1856]{1,...) custom-call(bf16[8,4096]{1,0:T(8,128)(2,1)} %go_hbm.1, ...), custom_call_target="tpu_custom_call" | custom-call | tf_op jit(solution)/shard_map/pallas_call | solution.py:449
  17.4 3.6 %shard_map.68 = (f32[1856,1024]{1,0:T(8,128)}, bf16[64,1856]{1,0:T(8,128)(2,1)}, bf16[64,1856]{1,0:T(8,128)(2,1)}) custom-call(bf16[256,1024]{1,0:T(8,128)(2,1)S(1)} %bitcast.5, bf16[256,1856]{1,0:T(8,128)(2,1)S(1)} %bitcast.4, f32[64,1856]{1,0:T(8,128)S(1)} %get-tuple-element.16.grad_ref, bf16[64,1856]{1,0:T(8,128)(2,1)S(1)} %get-tuple-element.17.other_ref, ...), custom_call_target="tpu_custom_call" | custom-call | tf_op jit(solution)/shard_map/pallas_call | solution.py:488
